TPU v7x, 32 devices: a whole 2x2x4 slice. The times are simulated.
32 devices in a mesh: dp: 4 (over z), mp: 8 (over y, x, core).
Axes of the slice: x: 2, y: 2, z: 4, core: 2. Of those that a mesh axis runs over, the one named last changes fastest.
Arguments:
- grad_parts: bfloat16 [4, 8, 2, 18432, 128], P('dp', 'mp'), may hold values from -45 to 45
- master: float32 [8, 2, 18432, 128], P('mp', None, 'dp'), may hold values from -15 to 15
- momenta: float32 [3, 8, 2, 18432, 128], P(None, 'mp', None, 'dp'), may hold values from -45 to 45
- second: float32 [3, 8, 2, 18432, 128], P(None, 'mp', None, 'dp'), may hold values from 0.00025 to 330
- step_count: int32 [1], replicated, may hold values from 1 to 99999
- mlp_first: float32 [8, 4], replicated, may hold values from -2 to 2
- mlp_bias: float32 [4], replicated, may hold values from -3 to 3
- mlp_second: float32 [4, 2], replicated, may hold values from -3 to 3
- tensor_weight: float32 [10], replicated, may hold values from -2 to 2
Outputs:
- new_params: bfloat16 [8, 2, 18432, 128], P('mp')
- new_master: float32 [8, 2, 18432, 128], P('mp', None, 'dp')
- new_momenta: float32 [3, 8, 2, 18432, 128], P(None, 'mp', None, 'dp')
- new_second: float32 [3, 8, 2, 18432, 128], P(None, 'mp', None, 'dp')
- update: float32 [8, 2, 18432, 128], P('mp', None, 'dp')
All inputs are finite; a program needn't handle non-finite values.
Results may differ from a plain program's by a relative error of at most 0.019.
Values may be sent and summed in bfloat16 or wider, within the bound.
A program may use at most 192 MiB of HBM per device.

v0:
```python
import functools

import jax
import jax.numpy as jnp
from jax import lax
from jax.experimental import pallas as pl
from jax.experimental.pallas import tpu as pltpu
from jax.sharding import PartitionSpec as P

D = 4608
HQ = 4096
RATES = (0.9, 0.99, 0.999)
MESH = pl.DeviceIdType.MESH
STRIP = 32


def block_rows(rows, most=1152):
    best = STRIP
    for size in range(STRIP, most + 1, STRIP):
        if rows % size == 0:
            best = size
    return best


def advanced(g, momenta, second):
    moments = [b * m + (1.0 - b) * g for b, m in zip(RATES, momenta)]
    gg = g * g
    squares = [b * s + (1.0 - b) * gg for b, s in zip(RATES, second)]
    return moments, squares


def listing_of(master, g, moments, squares):
    ratios = [m * lax.rsqrt(s) for m, s in zip(moments, squares)]
    return [master, g, *moments, *ratios]


def update_of(listing, coef, base, feats, hidden):
    direction = None
    magnitude = None
    tail = base + feats * hidden
    for j in range(hidden):
        active = listing[0] * coef[base + j] + coef[tail + j]
        for f in range(1, feats):
            active = active + listing[f] * coef[base + f * hidden + j]
        active = jnp.maximum(active, 0.0)
        d = active * coef[tail + hidden + j]
        m = active * coef[tail + 2 * hidden + j]
        direction = d if direction is None else direction + d
        magnitude = m if magnitude is None else magnitude + m
    return direction * jnp.exp(0.5 * jnp.tanh(magnitude))


def stats_kernel(steps, g_ref, master_ref, mom_ref, sec_ref, *rest):
    out_ref, acc = rest[-2:]
    i = pl.program_id(0)

    @pl.when(i == 0)
    def _():
        acc[...] = jnp.zeros_like(acc)

    def body(k, carry):
        rows = pl.ds(pl.multiple_of(k * STRIP, STRIP), STRIP)
        g = g_ref[rows, :].astype(jnp.float32)
        moments, squares = advanced(
            g, [mom_ref[c, 0, 0, rows, :] for c in range(3)], [sec_ref[c, 0, 0, rows, :] for c in range(3)]
        )
        feats = listing_of(master_ref[0, 0, rows, :], g, moments, squares)
        return tuple(
            a + jnp.sum((f * f).reshape(STRIP // 8, 8, 128), axis=0) for a, f in zip(carry, feats)
        )

    sums = lax.fori_loop(0, g_ref.shape[0] // STRIP, body, tuple(acc[f] for f in range(8)))
    for f in range(8):
        acc[f] = sums[f]

    @pl.when(i == steps - 1)
    def _():
        for f in range(8):
            out_ref[pl.ds(f, 1), :] = jnp.sum(acc[f], axis=0, keepdims=True)


def state_specs(rows, t_of):
    return [
        pl.BlockSpec((1, 1, rows, 128), lambda *a: (0, t_of(a), a[-1], 0)),
        pl.BlockSpec((3, 1, 1, rows, 128), lambda *a: (0, 0, t_of(a), a[-1], 0)),
        pl.BlockSpec((3, 1, 1, rows, 128), lambda *a: (0, 0, t_of(a), a[-1], 0)),
    ]


def cost(elements, flops, nbytes):
    return pl.CostEstimate(flops=elements * flops, bytes_accessed=nbytes, transcendentals=5 * elements)


def stats(t, g, master, momenta, second, after=()):
    own = g.shape[0]
    rows = block_rows(own)
    steps = own // rows
    return pl.pallas_call(
        functools.partial(stats_kernel, steps),
        grid=(steps,),
        out_shape=jax.ShapeDtypeStruct((8, 128), jnp.float32),
        in_specs=[pl.BlockSpec((rows, 128), lambda i: (i, 0))] + state_specs(rows, lambda a: t)
        + [pl.BlockSpec(memory_space=pl.ANY)] * len(after),
        out_specs=pl.BlockSpec((8, 128), lambda i: (0, 0)),
        scratch_shapes=[pltpu.VMEM((8, 8, 128), jnp.float32)],
        cost_estimate=cost(own * 128, 40, own * 128 * 30),
        name=f"stats{t}",
    )(g, master, momenta, second, *after)


def params_kernel(feats, hidden, coef, g_ref, master_ref, mom_ref, sec_ref, out_ref):
    def body(k, carry):
        rows = pl.ds(pl.multiple_of(k * STRIP, STRIP), STRIP)
        g = g_ref[rows, :].astype(jnp.float32)
        moments, squares = advanced(
            g, [mom_ref[c, 0, 0, rows, :] for c in range(3)], [sec_ref[c, 0, 0, rows, :] for c in range(3)]
        )
        master = master_ref[0, 0, rows, :]
        update = update_of(listing_of(master, g, moments, squares), coef, 0, feats, hidden)
        out_ref[rows, :] = (master - 0.05 * update).astype(jnp.bfloat16)
        return carry

    lax.fori_loop(0, g_ref.shape[0] // STRIP, body, 0)


def params(t, feats, hidden, coef, g, master, momenta, second):
    own = g.shape[0]
    rows = block_rows(own)
    return pl.pallas_call(
        functools.partial(params_kernel, feats, hidden),
        grid=(own // rows,),
        out_shape=jax.ShapeDtypeStruct((own, 128), jnp.bfloat16),
        in_specs=[pl.BlockSpec(memory_space=pltpu.SMEM), pl.BlockSpec((rows, 128), lambda i: (i, 0))]
        + state_specs(rows, lambda a: t),
        out_specs=pl.BlockSpec((rows, 128), lambda i: (i, 0)),
        cost_estimate=cost(own * 128, 130, own * 128 * 32),
        name=f"params{t}",
    )(coef, g, master, momenta, second)


def finish_kernel(
    feats, hidden, width, coef, g0_ref, g1_ref, master_ref, mom_ref, sec_ref, nm_ref, nmom_ref, nsec_ref, up_ref
):
    t = pl.program_id(0)
    base = t * width

    def body(k, carry):
        rows = pl.ds(pl.multiple_of(k * STRIP, STRIP), STRIP)
        g = jnp.where(t == 0, g0_ref[rows, :].astype(jnp.float32), g1_ref[rows, :].astype(jnp.float32))
        moments, squares = advanced(
            g, [mom_ref[c, 0, 0, rows, :] for c in range(3)], [sec_ref[c, 0, 0, rows, :] for c in range(3)]
        )
        for c in range(3):
            nmom_ref[c, 0, 0, rows, :] = moments[c]
            nsec_ref[c, 0, 0, rows, :] = squares[c]
        master = master_ref[0, 0, rows, :]
        update = update_of(listing_of(master, g, moments, squares), coef, base, feats, hidden)
        up_ref[0, 0, rows, :] = update
        nm_ref[0, 0, rows, :] = master - 0.05 * update
        return carry

    lax.fori_loop(0, g0_ref.shape[0] // STRIP, body, 0)


def finish(feats, hidden, coefs, g0, g1, master, momenta, second):
    own = g0.shape[0]
    rows = block_rows(own)
    steps = own // rows
    width = coefs.shape[0] // 2
    specs = state_specs(rows, lambda a: a[0])
    return pl.pallas_call(
        functools.partial(finish_kernel, feats, hidden, width),
        grid=(2, steps),
        out_shape=(
            jax.ShapeDtypeStruct(master.shape, jnp.float32),
            jax.ShapeDtypeStruct(momenta.shape, jnp.float32),
            jax.ShapeDtypeStruct(second.shape, jnp.float32),
            jax.ShapeDtypeStruct(master.shape, jnp.float32),
        ),
        in_specs=[
            pl.BlockSpec(memory_space=pltpu.SMEM),
            pl.BlockSpec((rows, 128), lambda t, i: (i * (1 - t) + (steps - 1) * t, 0)),
            pl.BlockSpec((rows, 128), lambda t, i: (i * t, 0)),
        ]
        + specs,
        out_specs=(specs[0], specs[1], specs[2], specs[0]),
        cost_estimate=cost(2 * own * 128, 130, 2 * own * 128 * 62),
        name="finish",
    )(coefs, g0, g1, master, momenta, second)


def total_kernel(n_dp, n_mp, x_ref, out_ref, near, far, send1, recv1, send2, recv2, local_sem):
    z = lax.axis_index("dp")
    m = lax.axis_index("mp")
    mine = pltpu.make_async_copy(x_ref, near.at[0], local_sem)
    mine.start()
    barrier = pltpu.get_barrier_semaphore()
    for j in range(1, n_mp):
        pl.semaphore_signal(barrier, inc=1, device_id=(z, lax.rem(m + j, n_mp)), device_id_type=MESH)
    for j in range(1, n_dp):
        pl.semaphore_signal(barrier, inc=1, device_id=(lax.rem(z + j, n_dp), m), device_id_type=MESH)
    pl.semaphore_wait(barrier, n_mp - 1 + n_dp - 1)
    first = []
    for j in range(1, n_mp):
        copy = pltpu.make_async_remote_copy(
            src_ref=x_ref,
            dst_ref=near.at[j],
            send_sem=send1.at[j],
            recv_sem=recv1.at[j],
            device_id=(z, lax.rem(m + j, n_mp)),
            device_id_type=MESH,
        )
        copy.start()
        first.append(copy)
    mine.wait()
    for copy in first:
        copy.wait()
    second = []
    for j in range(1, n_dp):
        copy = pltpu.make_async_remote_copy(
            src_ref=near,
            dst_ref=far.at[j - 1],
            send_sem=send2.at[j],
            recv_sem=recv2.at[j],
            device_id=(lax.rem(z + j, n_dp), m),
            device_id_type=MESH,
        )
        copy.start()
        second.append(copy)
    for copy in second:
        copy.wait()
    total = jnp.sum(near[...], axis=0)
    for j in range(n_dp - 1):
        total = total + jnp.sum(far[j], axis=0)
    out_ref[...] = total


def total(which, n_dp, n_mp, x):
    return pl.pallas_call(
        functools.partial(total_kernel, n_dp, n_mp),
        out_shape=jax.ShapeDtypeStruct(x.shape, x.dtype),
        in_specs=[pl.BlockSpec(memory_space=pltpu.VMEM)],
        out_specs=pl.BlockSpec(memory_space=pltpu.VMEM),
        scratch_shapes=[
            pltpu.VMEM((n_mp,) + x.shape, x.dtype),
            pltpu.VMEM((n_dp - 1, n_mp) + x.shape, x.dtype),
            pltpu.SemaphoreType.DMA((n_mp,)),
            pltpu.SemaphoreType.DMA((n_mp,)),
            pltpu.SemaphoreType.DMA((n_dp,)),
            pltpu.SemaphoreType.DMA((n_dp,)),
            pltpu.SemaphoreType.DMA,
        ],
        compiler_params=pltpu.CompilerParams(collective_id=which, has_side_effects=True),
        cost_estimate=pl.CostEstimate(flops=1000, bytes_accessed=10_000_000, transcendentals=0),
        name=f"total{which}",
    )(x)


def coef_kernel(totals_ref, step_ref, first_ref, bias_ref, second_ref, weight_ref, out_ref):
    feats, hidden = first_ref.shape
    sums = jnp.sum(totals_ref[...], axis=1, keepdims=True) + jnp.zeros((feats, 128), jnp.float32)
    norms = jnp.sqrt(sums / float(D * HQ) + 1e-06)
    logs = jnp.log(norms)
    inverse = 1.0 / norms
    step = jnp.full((1, 128), step_ref[0].astype(jnp.float32))
    logits = weight_ref[feats] * (jnp.log(1.0 + step) / 11.5) + weight_ref[feats + 1] * (step / 100000.0)
    for f in range(feats):
        logits = logits + weight_ref[f] * logs[f : f + 1, :]
    boost = jnp.exp(jnp.tanh(logits))[0, 0]
    for f in range(feats):
        scale = inverse[f, 0]
        for j in range(hidden):
            out_ref[f * hidden + j] = first_ref[f, j] * scale
    tail = feats * hidden
    for j in range(hidden):
        out_ref[tail + j] = bias_ref[j]
        out_ref[tail + hidden + j] = second_ref[j, 0] * boost
        out_ref[tail + 2 * hidden + j] = second_ref[j, 1]


def coefficients(totals, step_count, mlp_first, mlp_bias, mlp_second, tensor_weight):
    feats, hidden = mlp_first.shape
    smem = pl.BlockSpec(memory_space=pltpu.SMEM)
    return pl.pallas_call(
        coef_kernel,
        out_shape=jax.ShapeDtypeStruct(((feats + 3) * hidden,), jnp.float32),
        in_specs=[pl.BlockSpec(memory_space=pltpu.VMEM)] + [smem] * 5,
        out_specs=smem,
        name="coefficients",
    )(totals, step_count, mlp_first, mlp_bias, mlp_second, tensor_weight)


def pick_kernel(x_ref, out_ref):
    out_ref[...] = x_ref[0, 0, 0]


def pick(t, grad_parts):
    total_rows = grad_parts.shape[3]
    rows = block_rows(total_rows, 4608)
    return pl.pallas_call(
        pick_kernel,
        grid=(total_rows // rows,),
        out_shape=jax.ShapeDtypeStruct(grad_parts.shape[3:], grad_parts.dtype),
        in_specs=[pl.BlockSpec((1, 1, 1, rows, 128), lambda i: (0, 0, t, i, 0))],
        out_specs=pl.BlockSpec((rows, 128), lambda i: (i, 0)),
        cost_estimate=pl.CostEstimate(flops=0, bytes_accessed=4 * total_rows * 128, transcendentals=0),
        name=f"pick{t}",
    )(grad_parts)


def local(
    n_dp, n_mp, grad_parts, master, momenta, second, step_count, mlp_first, mlp_bias, mlp_second, tensor_weight
):
    feats, hidden = mlp_first.shape
    net = (step_count, mlp_first, mlp_bias, mlp_second, tensor_weight)
    g0 = lax.psum_scatter(pick(0, grad_parts), "dp", scatter_dimension=0, tiled=True)
    g0, part1 = lax.optimization_barrier((g0, pick(1, grad_parts)))
    g1 = lax.psum_scatter(part1, "dp", scatter_dimension=0, tiled=True)
    coef0 = coefficients(total(0, n_dp, n_mp, stats(0, g0, master, momenta, second)), *net)
    p0 = params(0, feats, hidden, coef0, g0, master, momenta, second)
    full0 = lax.all_gather(p0, "dp", axis=0, tiled=True)
    coef1 = coefficients(total(1, n_dp, n_mp, stats(1, g1, master, momenta, second, (p0,))), *net)
    p1 = params(1, feats, hidden, coef1, g1, master, momenta, second)
    full1 = lax.all_gather(p1, "dp", axis=0, tiled=True)
    new_master, new_momenta, new_second, update = finish(
        feats, hidden, jnp.concatenate([coef0, coef1]), g0, g1, master, momenta, second
    )
    out = jnp.stack([full0, full1])[None]
    return (out, new_master, new_momenta, new_second, update)


def solution(mesh):
    placed = (
        P("dp", "mp", None, None, None),
        P("mp", None, "dp", None),
        P(None, "mp", None, "dp", None),
        P(None, "mp", None, "dp", None),
        P(),
        P(),
        P(),
        P(),
        P(),
    )
    return jax.shard_map(
        functools.partial(local, mesh.shape["dp"], mesh.shape["mp"]),
        mesh=mesh,
        in_specs=placed,
        out_specs=(
            P("mp", None, None, None),
            P("mp", None, "dp", None),
            P(None, "mp", None, "dp", None),
            P(None, "mp", None, "dp", None),
            P("mp", None, "dp", None),
        ),
        check_vma=False,
    )
```

profile of v0, /device:TPU:0, one launch (start us, length us, event | category | flops | bytes accessed | tf_op | source)
XLA Modules:
  0.0 390.9 jit_solution(6471757492708821159)
XLA Ops:
  7.2 0.0 reduce-scatter.3.cloned.1.call-start
  7.2 5.0 %pick0.1 = bf16[18432,128]{1,0:T(8,128)(2,1)} custom-call(bf16[1,1,2,18432,128]{4,3,2,1,0:T(8,128)(2,1)} %x_ref.3), custom_call_target="tpu_custom_call" | custom-call | bytes 9437184 | tf_op jit(solution)/shard_map/pick0/pallas_call | solution.py:300
  12.2 0.0 reduce-scatter.3.cloned.1.call-update
  12.3 0.0 reduce-scatter.5.cloned.1.call-start
  12.3 5.0 %pick1.1 = bf16[18432,128]{1,0:T(8,128)(2,1)} custom-call(bf16[1,1,2,18432,128]{4,3,2,1,0:T(8,128)(2,1)} %x_ref.3), custom_call_target="tpu_custom_call" | custom-call | bytes 9437184 | tf_op jit(solution)/shard_map/pick1/pallas_call | solution.py:300
  17.4 83.1 %reduce-scatter.3.cloned.1.call-done.g_ref.g0_ref = bf16[4608,128]{1,0:T(8,128)(2,1)} async-done(((bf16[18432,128]{1,0:T(8,128)(2,1)}), bf16[4608,128]{1,0:T(8,128)(2,1)}) %reduce-scatter.3.cloned.1.call-update) | async-done | bytes 1179664 | tf_op jit(solution)/shard_map/reduce_scatter | solution.py:316
  100.5 0.0 all-gather.3.cloned.1.call-start
  101.2 0.7 copy.15.second_ref
  101.8 8.9 %stats0.1.x_ref = f32[8,128]{1,0:T(8,128)} custom-call(bf16[4608,128]{1,0:T(8,128)(2,1)} %reduce-scatter.3.cloned.1.call-done.g_ref.g0_ref, f32[1,2,4608,128]{3,2,1,0:T(8,128)} %master_ref.9, f32[3,1,2,4608,128]{4,3,2,1,0:T(8,128)} %mom_ref.9, f32[3,1,2,4608,128]{4,3,2,1,0:T(8,128)} %sec_ref.9), custom_call_target="tpu_custom_call" | custom-call | flops 23592960 | bytes 17694720 | tf_op jit(solution)/shard_map/stats0/pallas_call | solution.py:98
  110.8 0.7 copy.14.first_ref
  111.4 15.6 %total0.1.totals_ref = f32[8,128]{1,0:T(8,128)} custom-call(f32[8,128]{1,0:T(8,128)} %stats0.1.x_ref), custom_call_target="tpu_custom_call" | custom-call | flops 1000 | bytes 10000000 | tf_op jit(solution)/shard_map/total0/pallas_call | solution.py:239
  127.0 1.6 coefficients.2.coef
  128.6 15.9 %params0.1.rest_0_ = bf16[4608,128]{1,0:T(8,128)(2,1)} custom-call(f32[44]{0:T(128)} %coefficients.2.coef, bf16[4608,128]{1,0:T(8,128)(2,1)} %reduce-scatter.3.cloned.1.call-done.g_ref.g0_ref, f32[1,2,4608,128]{3,2,1,0:T(8,128)} %master_ref.9, f32[3,1,2,4608,128]{4,3,2,1,0:T(8,128)} %mom_ref.9, f32[3,1,2,4608,128]{4,3,2,1,0:T(8,128)} %sec_ref.9), custom_call_target="tpu_custom_call" | custom-call | flops 76677120 | bytes 18874368 | tf_op jit(solution)/shard_map/params0/pallas_call | solution.py:129
  144.6 0.0 all-gather.5.cloned.1.call-start
  144.6 46.6 %reduce-scatter.5.cloned.1.call-done.g_ref.g1_ref = bf16[4608,128]{1,0:T(8,128)(2,1)} async-done(((bf16[18432,128]{1,0:T(8,128)(2,1)}), bf16[4608,128]{1,0:T(8,128)(2,1)}) %reduce-scatter.5.cloned.1.call-update) | async-done | bytes 1179664 | tf_op jit(solution)/shard_map/reduce_scatter | solution.py:318
  191.3 8.9 %stats1.1.x_ref = f32[8,128]{1,0:T(8,128)} custom-call(bf16[4608,128]{1,0:T(8,128)(2,1)} %reduce-scatter.5.cloned.1.call-done.g_ref.g1_ref, f32[1,2,4608,128]{3,2,1,0:T(8,128)} %master_ref.9, f32[3,1,2,4608,128]{4,3,2,1,0:T(8,128)} %mom_ref.9, f32[3,1,2,4608,128]{4,3,2,1,0:T(8,128)} %sec_ref.9, bf16[4608,128]{1,0:T(8,128)(2,1)} %params0.1.rest_0_), custom_call_target="tpu_custom_call" | custom-call | flops 23592960 | bytes 17694720 | tf_op jit(solution)/shard_map/stats1/pallas_call | solution.py:98
  200.2 14.3 %total1.1.totals_ref = f32[8,128]{1,0:T(8,128)} custom-call(f32[8,128]{1,0:T(8,128)} %stats1.1.x_ref), custom_call_target="tpu_custom_call" | custom-call | flops 1000 | bytes 10000000 | tf_op jit(solution)/shard_map/total1/pallas_call | solution.py:239
  214.5 1.6 coefficients.3.coef
  216.1 15.9 %params1.1 = bf16[4608,128]{1,0:T(8,128)(2,1)} custom-call(f32[44]{0:T(128)} %coefficients.3.coef, bf16[4608,128]{1,0:T(8,128)(2,1)} %reduce-scatter.5.cloned.1.call-done.g_ref.g1_ref, f32[1,2,4608,128]{3,2,1,0:T(8,128)} %master_ref.9, f32[3,1,2,4608,128]{4,3,2,1,0:T(8,128)} %mom_ref.9, f32[3,1,2,4608,128]{4,3,2,1,0:T(8,128)} %sec_ref.9), custom_call_target="tpu_custom_call" | custom-call | flops 76677120 | bytes 18874368 | tf_op jit(solution)/shard_map/params1/pallas_call | solution.py:129
  232.1 0.7 pad_maximum_fusion.coef
  232.7 33.8 %finish.1 = (f32[1,2,4608,128]{3,2,1,0:T(8,128)}, f32[3,1,2,4608,128]{4,3,2,1,0:T(8,128)}, f32[3,1,2,4608,128]{4,3,2,1,0:T(8,128)}, f32[1,2,4608,128]{3,2,1,0:T(8,128)}) custom-call(f32[88]{0:T(128)} %pad_maximum_fusion.coef, bf16[4608,128]{1,0:T(8,128)(2,1)} %reduce-scatter.3.cloned.1.call-done.g_ref.g0_ref, ...), custom_call_target="tpu_custom_call" | custom-call | flops 153354240 | bytes 73138176 | tf_op jit(solution)/shard_map/finish/pallas_call | solution.py:171
  266.5 19.6 %all-gather.3.cloned.1.call-done = bf16[18432,128]{1,0:T(8,128)(2,1)} async-done(((bf16[4608,128]{1,0:T(8,128)(2,1)}), bf16[18432,128]{1,0:T(8,128)(2,1)}) %all-gather.3.cloned.1.call-update) | async-done | bytes 4718608 | tf_op jit(solution)/shard_map/all_gather | solution.py:321
  286.2 89.1 %all-gather.5.cloned.1.call-done = bf16[18432,128]{1,0:T(8,128)(2,1)} async-done(((bf16[4608,128]{1,0:T(8,128)(2,1)}), bf16[18432,128]{1,0:T(8,128)(2,1)}) %all-gather.5.cloned.1.call-update) | async-done | bytes 4718608 | tf_op jit(solution)/shard_map/all_gather | solution.py:324
  375.2 9.1 %maximum_bitcast_fusion = bf16[1,2,18432,128]{3,2,1,0:T(8,128)(2,1)} fusion(bf16[1,18432,128]{2,1,0:T(8,128)(2,1)} %bitcast.5, bf16[1,18432,128]{2,1,0:T(8,128)(2,1)} %bitcast.4), kind=kLoop, calls=%fused_computation | loop fusion | flops 4718592 | bytes 18874368 | tf_op jit(solution)/shard_map/broadcast_in_dim | solution.py:328
  (11 shorter events, 0.1 us)
Async XLA Ops:
  7.2 93.3 %reduce-scatter.3.cloned.1.call-start = ((), (), s32[]{:S(2)}) async-start(), calls=%async_computation.2 | async-start | bytes 5898240 | tf_op jit(solution)/shard_map/reduce_scatter | solution.py:316
  12.3 179.0 %reduce-scatter.5.cloned.1.call-start = ((), (), s32[]{:S(2)}) async-start(), calls=%async_computation.4 | async-start | bytes 5898240 | tf_op jit(solution)/shard_map/reduce_scatter | solution.py:318
  17.4 83.8 %copy-start.3 = (f32[4,2]{0,1:T(2,128)S(1)}, f32[4,2]{0,1:T(2,128)}, u32[]{:S(2)}) copy-start(f32[4,2]{0,1:T(2,128)} %param.16) | copy-start | bytes 100
  100.5 185.7 %all-gather.3.cloned.1.call-start = ((), (), s32[]{:S(2)}) async-start(), calls=%async_computation.3 | async-start | bytes 5898240 | tf_op jit(solution)/shard_map/all_gather | solution.py:321
  101.8 8.9 %copy-start.2 = (f32[8,4]{0,1:T(4,128)S(1)}, f32[8,4]{0,1:T(4,128)}, u32[]{:S(2)}) copy-start(f32[8,4]{0,1:T(4,128)} %param.14) | copy-start | bytes 388
  144.6 230.7 %all-gather.5.cloned.1.call-start = ((), (), s32[]{:S(2)}) async-start(), calls=%async_computation.5 | async-start | bytes 5898240 | tf_op jit(solution)/shard_map/all_gather | solution.py:324
  216.1 16.0 %copy-start = (f32[44]{0:T(128)S(1)}, f32[44]{0:T(128)}, u32[]{:S(2)}) copy-start(f32[44]{0:T(128)} %coefficients.2.coef) | copy-start | bytes 532
  216.1 16.0 %copy-start.1 = (f32[44]{0:T(128)S(1)}, f32[44]{0:T(128)}, u32[]{:S(2)}) copy-start(f32[44]{0:T(128)} %coefficients.3.coef) | copy-start | bytes 532
Sparse Core Ops, SparseCore 0:
  12.4 88.0 reduce-scatter.2
  103.3 87.8 reduce-scatter.4
  193.4 92.6 all-gather.2
  287.6 87.6 all-gather.4
where the time goes:
time: 391 us
  waiting for transfers between devices  239 us (61%)
  Pallas kernels  127 us (32%)
  between operations  14.5 us (4%)
  other arithmetic  9.76 us (2%)
    all_gather x1, waiting for transfers between devices, local(): full1 = lax.all_gather(p1, 'dp', axis=0, tiled=True)  89.1 us
    reduce_scatter x1, waiting for transfers between devices, local(): lax.psum_scatter(pick(0, grad_parts), 'dp', scatter_dimension=0, tiled=True)  83.1 us
    reduce_scatter x1, waiting for transfers between devices, local(): g1 = lax.psum_scatter(part1, 'dp', scatter_dimension=0, tiled=True)  46.6 us
    pallas_call x1, Pallas kernels, finish(): pl.pallas_call(functools.partial(finish_kernel, feats, hidden, width), gr...  33.8 us
    pallas_call x2, Pallas kernels, params(): pl.pallas_call(functools.partial(params_kernel, feats, hidden), grid=(own...  31.8 us
    pallas_call x2, Pallas kernels, total(): pl.pallas_call(functools.partial(total_kernel, n_dp, n_mp), out_shape=jax...  29.8 us
    all_gather x1, waiting for transfers between devices, local(): full0 = lax.all_gather(p0, 'dp', axis=0, tiled=True)  19.6 us
    pallas_call x2, Pallas kernels, stats(): pl.pallas_call(functools.partial(stats_kernel, steps), grid=(steps,), out...  17.8 us
  transfers between devices with their start and end apart: 4, of which 4 were waited for; matrix products, arithmetic and copies ran while one was open for 1% of the time, Pallas kernels for 31%

commit v1 on v0

v1 whole, which is shorter than its diff:
```python
import functools

import jax
import jax.numpy as jnp
from jax import lax
from jax.experimental import pallas as pl
from jax.experimental.pallas import tpu as pltpu
from jax.sharding import PartitionSpec as P

RATES = (0.9, 0.99, 0.999)
MESH = pl.DeviceIdType.MESH
STRIP = 32
LAG = 3
DEPTH = 4


def block_rows(rows, most=1152):
    best = STRIP
    for size in range(STRIP, most + 1, STRIP):
        if rows % size == 0:
            best = size
    return best


def advanced(g, momenta, second):
    moments = [b * m + (1.0 - b) * g for b, m in zip(RATES, momenta)]
    gg = g * g
    squares = [b * s + (1.0 - b) * gg for b, s in zip(RATES, second)]
    return moments, squares


def listing_of(master, g, moments, squares):
    ratios = [m * lax.rsqrt(s) for m, s in zip(moments, squares)]
    return [master, g, *moments, *ratios]


def update_of(listing, coef, base, feats, hidden):
    direction = None
    magnitude = None
    tail = base + feats * hidden
    for j in range(hidden):
        active = listing[0] * coef[base + j] + coef[tail + j]
        for f in range(1, feats):
            active = active + listing[f] * coef[base + f * hidden + j]
        active = jnp.maximum(active, 0.0)
        d = active * coef[tail + hidden + j]
        m = active * coef[tail + 2 * hidden + j]
        direction = d if direction is None else direction + d
        magnitude = m if magnitude is None else magnitude + m
    return direction * jnp.exp(0.5 * jnp.tanh(magnitude))


def pieces_of(own):
    strips = own // STRIP
    return max(k for k in range(1, 17) if strips % k == 0)


class Plan:
    def __init__(self, n_dp, n_mp, own):
        self.n, self.m, self.own = n_dp, n_mp, own
        self.k = pieces_of(own)
        self.pr = own // self.k
        self.lag = min(LAG, self.k)
        self.late = (2 * n_dp - 1) * self.k + max(0, self.lag + 8 - self.k)
        self.nt = self.late + self.k
        s0 = (n_dp - 2) * self.k + self.lag
        self.stats = (s0, s0 + (n_dp - 1) * self.k)
        self.send1 = tuple(s + self.k for s in self.stats)
        self.send2 = tuple(s + 2 for s in self.send1)
        self.done = tuple(s + 4 for s in self.send2)
        self.params = tuple(s + 1 for s in self.done)
        self.end = max(self.nt + self.lag * (n_dp - 1) + DEPTH, self.params[1] + self.k + 1)


def either(T, ticks):
    return (T == ticks[0]) | (T == ticks[1]), jnp.where(T >= ticks[1], 1, 0)


def within(T, starts, length):
    t = jnp.where(T >= starts[1], 1, 0)
    k = T - jnp.where(T >= starts[1], starts[1], starts[0])
    return (k >= 0) & (k < length), t, jnp.clip(k, 0, length - 1)


def mega_kernel(
    plan, feats, hidden,
    grad_ref, master_ref, mom_ref, sec_ref, step_ref, first_ref, bias_ref, second_ref, weight_ref,
    full_ref, p1_ref, right_ref, left_ref, g_ref, coef,
    gbuf, rbuf, masters, moms, secs, pbuf, acc, tot, near, nsum, far,
    load_sem, state_sem, send_sem, recv_sem, near_s, near_r, far_s, far_r, out_sem,
):
    n, m_n, own, K, pr = plan.n, plan.m, plan.own, plan.k, plan.pr
    width = (feats + 3) * hidden
    z = lax.axis_index("dp")
    m = lax.axis_index("mp")
    sides = (right_ref, left_ref)

    def chunk_load(t, c):
        rows = pl.ds(pl.multiple_of(c * own, STRIP), own)
        return pltpu.make_async_copy(grad_ref.at[0, 0, t, rows], gbuf.at[t, rows], load_sem.at[t, c])

    def state_loads(t):
        return (
            pltpu.make_async_copy(master_ref.at[0, t], masters.at[t], state_sem.at[t, 0]),
            pltpu.make_async_copy(mom_ref.at[:, 0, t], moms.at[t], state_sem.at[t, 1]),
            pltpu.make_async_copy(sec_ref.at[:, 0, t], secs.at[t], state_sem.at[t, 2]),
        )

    order = []
    for i in range((n + 1) // 2):
        order += [n - 1 - i] + ([i] if i != n - 1 - i else [])
    for t in range(2):
        for c in order:
            chunk_load(t, c).start()
    for t in range(2):
        for copy in state_loads(t):
            copy.start()

    barrier = pltpu.get_barrier_semaphore()
    for j in range(1, m_n):
        pl.semaphore_signal(barrier, inc=1, device_id=(z, lax.rem(m + j, m_n)), device_id_type=MESH)
    for j in range(1, n):
        pl.semaphore_signal(barrier, inc=1, device_id=(lax.rem(z + j, n), m), device_id_type=MESH)
    pl.semaphore_wait(barrier, m_n - 1 + n - 1)

    def place_of(d, T):
        q = z if d == 0 else n - 1 - z
        tau = T - plan.lag * q
        active = (tau >= 0) & (tau < plan.nt)
        tau = jnp.clip(tau, 0, plan.nt - 1)
        late = tau >= plan.late
        active = active & (late | (tau < (2 * n - 1) * K))
        s, k = lax.div(tau, K), lax.rem(jnp.where(late, tau - plan.late, tau), K)
        mid = (s >= n - 1) & (tau < (2 * n - 1) * K)
        cp = jnp.where(mid, 2 * n - 2 - s, jnp.where(late, q, n - 1 - s))
        t = jnp.where(mid, 1, 0)
        c = cp if d == 0 else n - 1 - cp
        si = jnp.clip(n - 1 - cp, 0, n - 2)
        return q, tau, active, k, mid, late, cp, t, c, si

    def piece(base, k):
        return pl.ds(pl.multiple_of(base + k * pr, STRIP), pr)

    def remote(d, src, dst, tau):
        to = lax.rem(z + 1, n) if d == 0 else lax.rem(z + n - 1, n)
        return pltpu.make_async_remote_copy(
            src_ref=src, dst_ref=dst, send_sem=send_sem.at[d, lax.rem(tau, DEPTH)], recv_sem=recv_sem.at[d, tau],
            device_id=(to, m), device_id_type=MESH,
        )

    def tick(T, carry):
        for d in range(2):
            q, tau, active, k, mid, late, cp, t, c, si = place_of(d, T)
            slot = rbuf.at[d, t, si, piece(0, k)]
            landed = full_ref.at[piece(c * own, k)]

            @pl.when(active & (q > 0) & (cp >= q) & ~late)
            def _():
                remote(d, slot, slot, tau).wait_recv()

            @pl.when(active & mid & (cp < q))
            def _():
                remote(d, landed, landed, tau).wait_recv()

            @pl.when(active & late & (q > 0))
            def _():
                remote(d, sides[d].at[piece(0, k)], sides[d].at[piece(0, k)], tau).wait_recv()

            @pl.when(active & (cp > q) & (k == 0))
            def _():
                chunk_load(t, c).wait()

            @pl.when(active & (q > 0) & (cp > q))
            def _():
                rows = piece(0, k)
                rbuf[d, t, si, rows, :] = rbuf[d, t, si, rows, :] + gbuf[t, piece(c * own, k), :]

        for d in range(2):
            q, tau, active, k, mid, late, cp, t, c, si = place_of(d, T - DEPTH)
            slot = rbuf.at[d, t, si, piece(0, k)]

            @pl.when(active & (q < n - 1) & ((cp > q) | mid | late))
            def _():
                remote(d, slot, slot, tau).wait_send()

            q, tau, active, k, mid, late, cp, t, c, si = place_of(d, T)
            slot = rbuf.at[d, t, si, piece(0, k)]
            landed = full_ref.at[piece(c * own, k)]

            @pl.when(active & (cp > q) & (q == 0))
            def _():
                remote(d, gbuf.at[t, piece(c * own, k)], slot, tau).start()

            @pl.when(active & (cp > q) & (q > 0))
            def _():
                remote(d, slot, slot, tau).start()

            @pl.when(active & mid & (cp == q) & (q < n - 1))
            def _():
                remote(d, pbuf.at[0, piece(0, k)], landed, tau).start()

            @pl.when(active & mid & (cp < q) & (q < n - 1))
            def _():
                remote(d, landed, landed, tau).start()

            @pl.when(active & late & (q < n - 1))
            def _():
                remote(d, pbuf.at[1, piece(0, k)], sides[d].at[piece(0, k)], tau).start()

        for d in range(2):
            edge = 0 if d == 0 else n - 1

            @pl.when((z == edge) & (T < K))
            def _():
                rows = piece(0, jnp.minimum(T, K - 1))
                for t in range(2):
                    rbuf[d, t, n - 2, rows, :] = jnp.zeros((pr, 128), jnp.bfloat16)

        live, t, k = within(T, plan.stats, K)

        @pl.when(live & (k == 0))
        def _():
            for copy in state_loads(t):
                copy.wait()
            chunk_load(t, z).wait()
            acc[...] = jnp.zeros_like(acc)

        @pl.when(live)
        def _():
            side = [jnp.minimum(n - 1 - z, n - 2), jnp.minimum(z, n - 2)]

            def body(i, sums):
                rows = pl.ds(pl.multiple_of(k * pr + i * STRIP, STRIP), STRIP)
                mine = pl.ds(pl.multiple_of(z * own + k * pr + i * STRIP, STRIP), STRIP)
                g = gbuf[t, mine, :].astype(jnp.float32)
                for d in range(2):
                    g = g + rbuf[d, t, side[d], rows, :].astype(jnp.float32)
                g = g.astype(jnp.bfloat16)
                gbuf[t, mine, :] = g
                g = g.astype(jnp.float32)
                moments, squares = advanced(
                    g, [moms[t, c, rows, :] for c in range(3)], [secs[t, c, rows, :] for c in range(3)]
                )
                listing = listing_of(masters[t, rows, :], g, moments, squares)
                return tuple(
                    a + jnp.sum((f * f).reshape(STRIP // 8, 8, 128), axis=0) for a, f in zip(sums, listing)
                )

            sums = lax.fori_loop(0, pr // STRIP, body, tuple(acc[f] for f in range(8)))
            for f in range(8):
                acc[f] = sums[f]

        @pl.when(live & (k == K - 1))
        def _():
            for f in range(8):
                tot[t, pl.ds(f, 1), :] = jnp.sum(acc[f], axis=0, keepdims=True)

        def near_copy(t, j):
            return pltpu.make_async_remote_copy(
                src_ref=tot.at[t], dst_ref=near.at[t, j], send_sem=near_s.at[t, j], recv_sem=near_r.at[t, j],
                device_id=(z, lax.rem(m + j, m_n)), device_id_type=MESH,
            )

        def far_copy(t, j):
            return pltpu.make_async_remote_copy(
                src_ref=nsum.at[t], dst_ref=far.at[t, j], send_sem=far_s.at[t, j], recv_sem=far_r.at[t, j],
                device_id=(lax.rem(z + j, n), m), device_id_type=MESH,
            )

        live, t = either(T, plan.send1)

        @pl.when(live)
        def _():
            for j in range(1, m_n):
                near_copy(t, j).start()

        live, t = either(T, tuple(s - 1 for s in plan.send2))

        @pl.when(live)
        def _():
            for j in range(1, m_n):
                near_copy(t, j).wait()
            total = tot[t]
            for j in range(1, m_n):
                total = total + near[t, j]
            nsum[t] = total

        live, t = either(T, plan.send2)

        @pl.when(live)
        def _():
            for j in range(1, n):
                far_copy(t, j).start()

        live, t = either(T, plan.done)

        @pl.when(live)
        def _():
            for j in range(1, n):
                far_copy(t, j).wait()
            total = nsum[t]
            for j in range(1, n):
                total = total + far[t, j]
            base = t * width
            sums = jnp.sum(total, axis=1, keepdims=True) + jnp.zeros((feats, 128), jnp.float32)
            norms = jnp.sqrt(sums / float(m_n * n * own * 128) + 1e-06)
            logs = jnp.log(norms)
            inverse = 1.0 / norms
            step = jnp.full((1, 128), step_ref[0].astype(jnp.float32))
            logits = weight_ref[feats] * (jnp.log(1.0 + step) / 11.5) + weight_ref[feats + 1] * (step / 100000.0)
            for f in range(feats):
                logits = logits + weight_ref[f] * logs[f : f + 1, :]
            boost = jnp.exp(jnp.tanh(logits))[0, 0]
            for f in range(feats):
                scale = inverse[f, 0]
                for j in range(hidden):
                    coef[base + f * hidden + j] = first_ref[j, f] * scale
            tail = base + feats * hidden
            for j in range(hidden):
                coef[tail + j] = bias_ref[j]
                coef[tail + hidden + j] = second_ref[0, j] * boost
                coef[tail + 2 * hidden + j] = second_ref[1, j]

        live, t, k = within(T, plan.params, K)

        @pl.when(live)
        def _():
            def body(i, carry):
                rows = pl.ds(pl.multiple_of(k * pr + i * STRIP, STRIP), STRIP)
                mine = pl.ds(pl.multiple_of(z * own + k * pr + i * STRIP, STRIP), STRIP)
                g = gbuf[t, mine, :].astype(jnp.float32)
                moments, squares = advanced(
                    g, [moms[t, c, rows, :] for c in range(3)], [secs[t, c, rows, :] for c in range(3)]
                )
                master = masters[t, rows, :]
                update = update_of(listing_of(master, g, moments, squares), coef, t * width, feats, hidden)
                pbuf[t, rows, :] = (master - 0.05 * update).astype(jnp.bfloat16)
                return carry

            lax.fori_loop(0, pr // STRIP, body, 0)

        @pl.when(T == plan.params[0] + K)
        def _():
            out(0).start()

        @pl.when(T == plan.params[1] + K)
        def _():
            out(3).start()

        for t in range(2):

            @pl.when(T == plan.stats[t] + K)
            def _():
                out(1 + t).start()

        return carry

    def out(i):
        mine = pl.ds(pl.multiple_of(z * own, STRIP), own)
        src, dst = (
            (pbuf.at[0], full_ref.at[mine]),
            (gbuf.at[0, mine], g_ref.at[0]),
            (gbuf.at[1, mine], g_ref.at[1]),
            (pbuf.at[1], p1_ref),
        )[i]
        return pltpu.make_async_copy(src, dst, out_sem.at[i])

    lax.fori_loop(0, plan.end, tick, 0)
    for i in range(4):
        out(i).wait()


def mega(n_dp, n_mp, grad_parts, master, momenta, second, step_count, mlp_first, mlp_bias, mlp_second, tensor_weight):
    feats, hidden = mlp_first.shape
    own, total_rows = master.shape[2], grad_parts.shape[3]
    plan = Plan(n_dp, n_mp, own)
    width = (feats + 3) * hidden
    smem = pl.BlockSpec(memory_space=pltpu.SMEM)
    anywhere = pl.BlockSpec(memory_space=pl.ANY)
    sem = pltpu.SemaphoreType.DMA
    return pl.pallas_call(
        functools.partial(mega_kernel, plan, feats, hidden),
        out_shape=(
            jax.ShapeDtypeStruct((total_rows, 128), jnp.bfloat16),
            jax.ShapeDtypeStruct((own, 128), jnp.bfloat16),
            jax.ShapeDtypeStruct((own, 128), jnp.bfloat16),
            jax.ShapeDtypeStruct((own, 128), jnp.bfloat16),
            jax.ShapeDtypeStruct((2, own, 128), jnp.bfloat16),
            jax.ShapeDtypeStruct((2 * width,), jnp.float32),
        ),
        in_specs=[anywhere] * 4 + [smem] * 5,
        out_specs=(anywhere,) * 5 + (smem,),
        scratch_shapes=[
            pltpu.VMEM((2, total_rows, 128), jnp.bfloat16),
            pltpu.VMEM((2, 2, n_dp - 1, own, 128), jnp.bfloat16),
            pltpu.VMEM((2, own, 128), jnp.float32),
            pltpu.VMEM((2, 3, own, 128), jnp.float32),
            pltpu.VMEM((2, 3, own, 128), jnp.float32),
            pltpu.VMEM((2, own, 128), jnp.bfloat16),
            pltpu.VMEM((8, 8, 128), jnp.float32),
            pltpu.VMEM((2, feats, 128), jnp.float32),
            pltpu.VMEM((2, n_mp, feats, 128), jnp.float32),
            pltpu.VMEM((2, feats, 128), jnp.float32),
            pltpu.VMEM((2, n_dp, feats, 128), jnp.float32),
            sem((2, n_dp)),
            sem((2, 3)),
            sem((2, DEPTH)),
            sem((2, plan.nt)),
            sem((2, n_mp)),
            sem((2, n_mp)),
            sem((2, n_dp)),
            sem((2, n_dp)),
            sem((4,)),
        ],
        compiler_params=pltpu.CompilerParams(
            collective_id=0, has_side_effects=True, vmem_limit_bytes=67_000_000
        ),
        cost_estimate=pl.CostEstimate(flops=10**9, bytes_accessed=10**8, transcendentals=0),
        name="exchange",
    )(grad_parts, master, momenta, second, step_count, mlp_first.T, mlp_bias, mlp_second.T, tensor_weight)


def finish_kernel(t, feats, hidden, width, coef, g_ref, master_ref, mom_ref, sec_ref, *rest):
    nm_ref, nmom_ref, nsec_ref, up_ref = rest[-4:]

    def body(k, carry):
        rows = pl.ds(pl.multiple_of(k * STRIP, STRIP), STRIP)
        g = g_ref[0, rows, :].astype(jnp.float32)
        moments, squares = advanced(
            g, [mom_ref[c, 0, 0, rows, :] for c in range(3)], [sec_ref[c, 0, 0, rows, :] for c in range(3)]
        )
        for c in range(3):
            nmom_ref[c, 0, 0, rows, :] = moments[c]
            nsec_ref[c, 0, 0, rows, :] = squares[c]
        master = master_ref[0, 0, rows, :]
        update = update_of(listing_of(master, g, moments, squares), coef, t * width, feats, hidden)
        up_ref[0, 0, rows, :] = update
        nm_ref[0, 0, rows, :] = master - 0.05 * update
        return carry

    lax.fori_loop(0, g_ref.shape[1] // STRIP, body, 0)


def finish(t, feats, hidden, coefs, g, master, momenta, second, earlier=()):
    own = g.shape[1]
    rows = block_rows(own)
    specs = [
        pl.BlockSpec((1, 1, rows, 128), lambda i: (0, t, i, 0)),
        pl.BlockSpec((3, 1, 1, rows, 128), lambda i: (0, 0, t, i, 0)),
        pl.BlockSpec((3, 1, 1, rows, 128), lambda i: (0, 0, t, i, 0)),
    ]
    return pl.pallas_call(
        functools.partial(finish_kernel, t, feats, hidden, coefs.shape[0] // 2),
        grid=(own // rows,),
        out_shape=(
            jax.ShapeDtypeStruct(master.shape, jnp.float32),
            jax.ShapeDtypeStruct(momenta.shape, jnp.float32),
            jax.ShapeDtypeStruct(second.shape, jnp.float32),
            jax.ShapeDtypeStruct(master.shape, jnp.float32),
        ),
        in_specs=[
            pl.BlockSpec(memory_space=pltpu.SMEM),
            pl.BlockSpec((1, rows, 128), lambda i: (t, i, 0)),
        ]
        + specs
        + [pl.BlockSpec(memory_space=pl.ANY)] * len(earlier),
        out_specs=(specs[0], specs[1], specs[2], specs[0]),
        input_output_aliases={5 + i: i for i in range(len(earlier))},
        cost_estimate=pl.CostEstimate(
            flops=own * 128 * 130, bytes_accessed=own * 128 * 62, transcendentals=5 * own * 128
        ),
        name=f"finish{t}",
    )(coefs, g, master, momenta, second, *earlier)


def assemble_kernel(n_dp, own, full_ref, mine_ref, *rest):
    count = 2 * (n_dp - 2)
    others = rest[:count]
    out_ref, fbuf, buf, load_sem, store_sem = rest[count:]
    z = lax.axis_index("dp")
    moves = [(full_ref, fbuf, out_ref.at[0, 0], None)]
    moves.append((mine_ref, buf.at[0], out_ref.at[0, 1, pl.ds(pl.multiple_of(z * own, STRIP), own)], None))
    for i in range(count):
        c = z - (i // 2 + 1) if i % 2 == 0 else z + (i // 2 + 1)
        ok = (c >= 0) if i % 2 == 0 else (c < n_dp)
        at = pl.ds(pl.multiple_of(jnp.clip(c, 0, n_dp - 1) * own, STRIP), own)
        moves.append((others[i], buf.at[1 + i], out_ref.at[0, 1, at], ok))

    def each(act):
        for i, (src, mid, dst, ok) in enumerate(moves):
            load = pltpu.make_async_copy(src, mid, load_sem.at[i])
            store = pltpu.make_async_copy(mid, dst, store_sem.at[i])
            if ok is None:
                act(load, store)
            else:
                pl.when(ok)(functools.partial(act, load, store))

    each(lambda load, store: load.start())

    def forward(load, store):
        load.wait()
        store.start()

    each(forward)
    each(lambda load, store: store.wait())


def assemble(n_dp, full, mine, others):
    own = mine.shape[0]
    anywhere = pl.BlockSpec(memory_space=pl.ANY)
    count = 2 + len(others)
    return pl.pallas_call(
        functools.partial(assemble_kernel, n_dp, own),
        out_shape=jax.ShapeDtypeStruct((1, 2) + full.shape, full.dtype),
        in_specs=[anywhere] * count,
        out_specs=anywhere,
        scratch_shapes=[
            pltpu.VMEM(full.shape, full.dtype),
            pltpu.VMEM((count - 1,) + mine.shape, mine.dtype),
            pltpu.SemaphoreType.DMA((count,)),
            pltpu.SemaphoreType.DMA((count,)),
        ],
        cost_estimate=pl.CostEstimate(flops=10**7, bytes_accessed=4 * full.size, transcendentals=0),
        name="assemble",
    )(full, mine, *others)


def last_kernel(n_dp, own, right_ref, left_ref, _, out_ref, buf, sems):
    z = lax.axis_index("dp")
    for d, (src, row) in enumerate(((right_ref, 0), (left_ref, (n_dp - 1) * own))):

        @pl.when(z == (n_dp - 1 if d == 0 else 0))
        def _():
            load = pltpu.make_async_copy(src, buf, sems.at[0])
            load.start()
            load.wait()
            store = pltpu.make_async_copy(buf, out_ref.at[0, 1, pl.ds(row, own)], sems.at[1])
            store.start()
            store.wait()


def last(n_dp, right, left, out):
    anywhere = pl.BlockSpec(memory_space=pl.ANY)
    return pl.pallas_call(
        functools.partial(last_kernel, n_dp, right.shape[0]),
        out_shape=jax.ShapeDtypeStruct(out.shape, out.dtype),
        in_specs=[anywhere] * 3,
        out_specs=anywhere,
        input_output_aliases={2: 0},
        scratch_shapes=[pltpu.VMEM(right.shape, right.dtype), pltpu.SemaphoreType.DMA((2,))],
        name="last",
    )(right, left, out)


def local(
    n_dp, n_mp, grad_parts, master, momenta, second, step_count, mlp_first, mlp_bias, mlp_second, tensor_weight
):
    feats, hidden = mlp_first.shape
    full0, p1, right, left, g, coefs = mega(
        n_dp, n_mp, grad_parts, master, momenta, second, step_count, mlp_first, mlp_bias, mlp_second, tensor_weight
    )
    others = [right, left]
    state = ()
    for step in range(2, n_dp):
        sent = (right, left)
        right = lax.ppermute(sent[0], "dp", [(i, i + 1) for i in range(step - 1, n_dp - 1)])
        left = lax.ppermute(sent[1], "dp", [(i, i - 1) for i in range(1, n_dp - step + 1)])
        if step <= 3:
            state = finish(step - 2, feats, hidden, coefs, g, master, momenta, second, state)
        if step < n_dp - 1:
            right, left, state = lax.optimization_barrier((right, left, state))
            others += [right, left]
    out = last(n_dp, right, left, assemble(n_dp, full0, p1, others))
    return (out, *state)


def solution(mesh):
    placed = (
        P("dp", "mp", None, None, None),
        P("mp", None, "dp", None),
        P(None, "mp", None, "dp", None),
        P(None, "mp", None, "dp", None),
        P(),
        P(),
        P(),
        P(),
        P(),
    )
    return jax.shard_map(
        functools.partial(local, mesh.shape["dp"], mesh.shape["mp"]),
        mesh=mesh,
        in_specs=placed,
        out_specs=(
            P("mp", None, None, None),
            P("mp", None, "dp", None),
            P(None, "mp", None, "dp", None),
            P(None, "mp", None, "dp", None),
            P("mp", None, "dp", None),
        ),
        check_vma=False,
    )
```

time: 391 us -> 288 us (0.74)
  waiting for transfers between devices: 239 us -> 12.6 us
  Pallas kernels: 127 us -> 270 us
  between operations: 14.5 us -> 1.37 us
  other arithmetic: 9.76 us -> 0 us
    pallas_call x11 -> x5, Pallas kernels: 127 us -> 270 us  [the longest x1 224 us: mega(): pl.pallas_call(functools.partial(mega_kernel, plan, feats, hidden), out_s...]
    reduce_scatter x2 -> x0, waiting for transfers between devices: 130 us -> none  [the longest x1 83.1 us: local(): lax.psum_scatter(pick(0, grad_parts), 'dp', scatter_dimension=0, tiled=True)]
    all_gather x2 -> x0, waiting for transfers between devices: 109 us -> none  [the longest x1 89.1 us: local(): full1 = lax.all_gather(p1, 'dp', axis=0, tiled=True)]
    ppermute x0 -> x4, waiting for transfers between devices: none -> 12.6 us  [the longest x2 12.6 us: local(): lax.ppermute(sent[1], 'dp', [(i, i - 1) for i in range(1, n_dp - step + 1)])]
    broadcast_in_dim x1 -> x0, other arithmetic: 9.1 us -> none  [local(): out = jnp.stack([full0, full1])[None]]
    ppermute x0 -> x4, starting transfers between devices: none -> 4.05 us  [the longest x2 2.58 us: local(): lax.ppermute(sent[1], 'dp', [(i, i - 1) for i in range(1, n_dp - step + 1)])]
  transfers between devices with their start and end apart: 4 -> 4, of which waited for: 4 -> 2; matrix products, arithmetic and copies ran while one was open for 1% -> 0% of each run, Pallas kernels for 31% -> 15%
where the time goes in v1:
time: 288 us
  Pallas kernels  270 us (94%)
  waiting for transfers between devices  12.6 us (4%)
  starting transfers between devices  4.05 us (1%)
    pallas_call x1, Pallas kernels, mega(): pl.pallas_call(functools.partial(mega_kernel, plan, feats, hidden), out_s...  224 us
    pallas_call x2, Pallas kernels, finish(): pl.pallas_call(functools.partial(finish_kernel, t, feats, hidden, coefs.s...  37 us
    ppermute x2, waiting for transfers between devices, local(): lax.ppermute(sent[1], 'dp', [(i, i - 1) for i in range(1, n_dp - step + 1)])  12.6 us
  transfers between devices with their start and end apart: 4, of which 2 were waited for; matrix products, arithmetic and copies ran while one was open for 0% of the time, Pallas kernels for 15%

profile of v1, /device:TPU:0, one launch (start us, length us, event | category | flops | bytes accessed | tf_op | source)
XLA Modules:
  0.0 287.6 jit_solution(6984594314740198466)
XLA Ops:
  1.3 224.5 %exchange.1 = (bf16[18432,128]{1,0:T(8,128)(2,1)}, bf16[4608,128]{1,0:T(8,128)(2,1)}, bf16[4608,128]{1,0:T(8,128)(2,1)}, bf16[4608,128]{1,0:T(8,128)(2,1)}, bf16[2,4608,128]{2,1,0:T(8,128)(2,1)}, /*index=5*/f32[88]{0:T(128)}) custom-call(bf16[1,1,2,18432,128]{4,3,2,1,0:T(8,128)(2,1)} %grad_ref.1, f32[1,2,4608,128]{3,2,1,0:T(8,128)} %master_ref.5, ...), custom_call_target="tpu_custom_call" | custom-call | flops 1000000000 | bytes 100000000 | tf_op jit(solution)/shard_map/exchange/pallas_call | solution.py:381
  225.7 0.7 collective-permute-start
  226.5 1.3 collective-permute-start.1
  227.8 18.5 %finish0.1 = (f32[1,2,4608,128]{3,2,1,0:T(8,128)}, f32[3,1,2,4608,128]{4,3,2,1,0:T(8,128)}, f32[3,1,2,4608,128]{4,3,2,1,0:T(8,128)}, f32[1,2,4608,128]{3,2,1,0:T(8,128)}) custom-call(f32[88]{0:T(128)} %get-tuple-element.27.coef, bf16[2,4608,128]{2,1,0:T(8,128)(2,1)} %get-tuple-element.28.g_ref, f32[1,2,4608,128]{3,2,1,0:T(8,128)} %master_ref.5, ...), custom_call_target="tpu_custom_call" | custom-call | flops 76677120 | bytes 36569088 | tf_op jit(solution)/shard_map/finish0/pallas_call | solution.py:452
  246.3 0.0 collective-permute-done.rest_2_
  246.3 0.0 copy-start
  246.3 9.7 %collective-permute-done.1.rest_3_ = bf16[4608,128]{1,0:T(8,128)(2,1)S(1)} collective-permute-done((bf16[4608,128]{1,0:T(8,128)(2,1)}, bf16[4608,128]{1,0:T(8,128)(2,1)S(1)}, u32[]{:S(2)}, u32[]{:S(2)}) %collective-permute-start.1) | collective-permute-done | bytes 1179680 | tf_op jit(solution)/shard_map/ppermute | solution.py:567
  256.0 0.0 copy-start.1
  256.0 0.7 collective-permute-start.2
  256.7 1.3 collective-permute-start.3
  258.0 0.0 copy-done
  258.0 0.0 copy-done.1
  258.1 5.7 %assemble.1._ = bf16[1,2,18432,128]{3,2,1,0:T(8,128)(2,1)} custom-call(bf16[18432,128]{1,0:T(8,128)(2,1)} %get-tuple-element.35.full_ref, bf16[4608,128]{1,0:T(8,128)(2,1)} %get-tuple-element.36.mine_ref, bf16[4608,128]{1,0:T(8,128)(2,1)} %get-tuple-element.25.rest_0_, bf16[4608,128]{1,0:T(8,128)(2,1)} %get-tuple-element.26.rest_1_, ...), custom_call_target="tpu_custom_call" | custom-call | flops 10000000 | bytes 9437184 | tf_op jit(solution)/shard_map/assemble/pallas_call | solution.py:512
  263.8 18.5 %finish1.1 = (f32[1,2,4608,128]{3,2,1,0:T(8,128)}, f32[3,1,2,4608,128]{4,3,2,1,0:T(8,128)}, f32[3,1,2,4608,128]{4,3,2,1,0:T(8,128)}, f32[1,2,4608,128]{3,2,1,0:T(8,128)}) custom-call(f32[88]{0:T(128)} %get-tuple-element.27.coef, ...), custom_call_target="tpu_custom_call", output_to_operand_aliasing={{0}: (5, {}), {1}: (6, {}), {2}: (7, {}), {3}: (8, {})} | custom-call | flops 76677120 | bytes 36569088 | tf_op jit(solution)/shard_map/finish1/pallas_call | solution.py:452
  282.3 0.0 collective-permute-done.2.right_ref
  282.3 0.0 copy-start.2
  282.3 3.0 %collective-permute-done.3.left_ref = bf16[4608,128]{1,0:T(8,128)(2,1)} collective-permute-done((bf16[4608,128]{1,0:T(8,128)(2,1)S(1)}, bf16[4608,128]{1,0:T(8,128)(2,1)}, u32[]{:S(2)}, u32[]{:S(2)}) %collective-permute-start.3) | collective-permute-done | bytes 1179680 | tf_op jit(solution)/shard_map/ppermute | solution.py:567
  285.3 0.0 copy-done.2
  285.3 2.3 last.1
Async XLA Ops:
  225.7 20.6 %collective-permute-start = (bf16[4608,128]{1,0:T(8,128)(2,1)}, bf16[4608,128]{1,0:T(8,128)(2,1)S(1)}, u32[]{:S(2)}, u32[]{:S(2)}) collective-permute-start(bf16[4608,128]{1,0:T(8,128)(2,1)} %get-tuple-element.25.rest_0_), channel_id=1, source_target_pairs={{8,16},{16,24},{9,17},{17,25},{10,18},{18,26},{11,19},{19,27},{12,... | collective-permute-start | bytes 3538952 | tf_op jit(solution)/shard_map/ppermute | solution.py:566
  226.5 29.5 %collective-permute-start.1 = (bf16[4608,128]{1,0:T(8,128)(2,1)}, bf16[4608,128]{1,0:T(8,128)(2,1)S(1)}, u32[]{:S(2)}, u32[]{:S(2)}) collective-permute-start(bf16[4608,128]{1,0:T(8,128)(2,1)} %get-tuple-element.26.rest_1_), channel_id=1, source_target_pairs={{8,0},{16,8},{9,1},{17,9},{10,2},{18,10},{11,3},{19,11},{12,4},{20... | collective-permute-start | bytes 3538952 | tf_op jit(solution)/shard_map/ppermute | solution.py:567
  246.3 11.7 %copy-start = (bf16[4608,128]{1,0:T(8,128)(2,1)}, bf16[4608,128]{1,0:T(8,128)(2,1)S(1)}, u32[]{:S(2)}) copy-start(bf16[4608,128]{1,0:T(8,128)(2,1)S(1)} %collective-permute-done.rest_2_) | copy-start | bytes 3538948
  256.0 2.0 copy-start.1
  256.0 26.3 %collective-permute-start.2 = (bf16[4608,128]{1,0:T(8,128)(2,1)S(1)}, bf16[4608,128]{1,0:T(8,128)(2,1)S(1)}, u32[]{:S(2)}, u32[]{:S(2)}) collective-permute-start(bf16[4608,128]{1,0:T(8,128)(2,1)S(1)} %collective-permute-done.rest_2_), channel_id=1, source_target_pairs={{16,24},{17,25},{18,26},{19,27},{20,28},{21,29},{22,30},{23,31}} | collective-permute-start | bytes 3538952 | tf_op jit(solution)/shard_map/ppermute | solution.py:566
  256.7 28.6 %collective-permute-start.3 = (bf16[4608,128]{1,0:T(8,128)(2,1)S(1)}, bf16[4608,128]{1,0:T(8,128)(2,1)}, u32[]{:S(2)}, u32[]{:S(2)}) collective-permute-start(bf16[4608,128]{1,0:T(8,128)(2,1)S(1)} %collective-permute-done.1.rest_3_), channel_id=1, source_target_pairs={{8,0},{9,1},{10,2},{11,3},{12,4},{13,5},{14,6},{15,7}} | collective-permute-start | bytes 3538952 | tf_op jit(solution)/shard_map/ppermute | solution.py:567
  282.3 3.0 %copy-start.2 = (bf16[4608,128]{1,0:T(8,128)(2,1)}, bf16[4608,128]{1,0:T(8,128)(2,1)S(1)}, u32[]{:S(2)}) copy-start(bf16[4608,128]{1,0:T(8,128)(2,1)S(1)} %collective-permute-done.2.right_ref) | copy-start | bytes 3538948

commit v2 on v1

--- a/solution.py
+++ b/solution.py
@@ -12,6 +12,7 @@
 STRIP = 32
 LAG = 3
 DEPTH = 4
+MOST = 16
 
 
 def block_rows(rows, most=1152):
@@ -52,7 +53,7 @@
 
 def pieces_of(own):
     strips = own // STRIP
-    return max(k for k in range(1, 17) if strips % k == 0)
+    return max(k for k in range(1, MOST + 1) if strips % k == 0)
 
 
 class Plan:
@@ -69,6 +70,7 @@
         self.send2 = tuple(s + 2 for s in self.send1)
         self.done = tuple(s + 4 for s in self.send2)
         self.params = tuple(s + 1 for s in self.done)
+        self.gathered = (2 * n_dp - 1) * self.k + self.lag * (n_dp - 1)
         self.end = max(self.nt + self.lag * (n_dp - 1) + DEPTH, self.params[1] + self.k + 1)
 
 
@@ -86,7 +88,7 @@
     plan, feats, hidden,
     grad_ref, master_ref, mom_ref, sec_ref, step_ref, first_ref, bias_ref, second_ref, weight_ref,
     full_ref, p1_ref, right_ref, left_ref, g_ref, coef,
-    gbuf, rbuf, masters, moms, secs, pbuf, acc, tot, near, nsum, far,
+    gbuf, rbuf, masters, moms, secs, fbuf, pbuf, acc, tot, near, nsum, far,
     load_sem, state_sem, send_sem, recv_sem, near_s, near_r, far_s, far_r, out_sem,
 ):
     n, m_n, own, K, pr = plan.n, plan.m, plan.own, plan.k, plan.pr
@@ -94,6 +96,10 @@
     z = lax.axis_index("dp")
     m = lax.axis_index("mp")
     sides = (right_ref, left_ref)
+
+    def landing(d, receiver):
+        first = (receiver < n // 2) == (d == 0) if n == 4 else jnp.bool_(d == 0)
+        return first, ~first
 
     def chunk_load(t, c):
         rows = pl.ds(pl.multiple_of(c * own, STRIP), own)
@@ -152,7 +158,7 @@
         for d in range(2):
             q, tau, active, k, mid, late, cp, t, c, si = place_of(d, T)
             slot = rbuf.at[d, t, si, piece(0, k)]
-            landed = full_ref.at[piece(c * own, k)]
+            landed = fbuf.at[piece(c * own, k)]
 
             @pl.when(active & (q > 0) & (cp >= q) & ~late)
             def _():
@@ -162,9 +168,11 @@
             def _():
                 remote(d, landed, landed, tau).wait_recv()
 
-            @pl.when(active & late & (q > 0))
-            def _():
-                remote(d, sides[d].at[piece(0, k)], sides[d].at[piece(0, k)], tau).wait_recv()
+            for side, chosen in enumerate(landing(d, z)):
+
+                @pl.when(active & late & (q > 0) & chosen)
+                def _():
+                    remote(d, sides[side].at[piece(0, k)], sides[side].at[piece(0, k)], tau).wait_recv()
 
             @pl.when(active & (cp > q) & (k == 0))
             def _():
@@ -185,7 +193,7 @@
 
             q, tau, active, k, mid, late, cp, t, c, si = place_of(d, T)
             slot = rbuf.at[d, t, si, piece(0, k)]
-            landed = full_ref.at[piece(c * own, k)]
+            landed = fbuf.at[piece(c * own, k)]
 
             @pl.when(active & (cp > q) & (q == 0))
             def _():
@@ -195,17 +203,15 @@
             def _():
                 remote(d, slot, slot, tau).start()
 
-            @pl.when(active & mid & (cp == q) & (q < n - 1))
-            def _():
-                remote(d, pbuf.at[0, piece(0, k)], landed, tau).start()
-
-            @pl.when(active & mid & (cp < q) & (q < n - 1))
+            @pl.when(active & mid & (cp <= q) & (q < n - 1))
             def _():
                 remote(d, landed, landed, tau).start()
 
-            @pl.when(active & late & (q < n - 1))
-            def _():
-                remote(d, pbuf.at[1, piece(0, k)], sides[d].at[piece(0, k)], tau).start()
+            for side, chosen in enumerate(landing(d, z + 1 if d == 0 else z - 1)):
+
+                @pl.when(active & late & (q < n - 1) & chosen)
+                def _():
+                    remote(d, pbuf.at[piece(0, k)], sides[side].at[piece(0, k)], tau).start()
 
         for d in range(2):
             edge = 0 if d == 0 else n - 1
@@ -323,8 +329,7 @@
 
         live, t, k = within(T, plan.params, K)
 
-        @pl.when(live)
-        def _():
+        def params(fresh, at):
             def body(i, carry):
                 rows = pl.ds(pl.multiple_of(k * pr + i * STRIP, STRIP), STRIP)
                 mine = pl.ds(pl.multiple_of(z * own + k * pr + i * STRIP, STRIP), STRIP)
@@ -334,12 +339,21 @@
                 )
                 master = masters[t, rows, :]
                 update = update_of(listing_of(master, g, moments, squares), coef, t * width, feats, hidden)
-                pbuf[t, rows, :] = (master - 0.05 * update).astype(jnp.bfloat16)
+                to = pl.ds(pl.multiple_of(at + k * pr + i * STRIP, STRIP), STRIP)
+                fresh[to, :] = (master - 0.05 * update).astype(jnp.bfloat16)
                 return carry
 
             lax.fori_loop(0, pr // STRIP, body, 0)
 
-        @pl.when(T == plan.params[0] + K)
+        @pl.when(live & (t == 0))
+        def _():
+            params(fbuf, z * own)
+
+        @pl.when(live & (t == 1))
+        def _():
+            params(pbuf, 0)
+
+        @pl.when(T == plan.gathered)
         def _():
             out(0).start()
 
@@ -358,10 +372,10 @@
     def out(i):
         mine = pl.ds(pl.multiple_of(z * own, STRIP), own)
         src, dst = (
-            (pbuf.at[0], full_ref.at[mine]),
+            (fbuf, full_ref),
             (gbuf.at[0, mine], g_ref.at[0]),
             (gbuf.at[1, mine], g_ref.at[1]),
-            (pbuf.at[1], p1_ref),
+            (pbuf, p1_ref),
         )[i]
         return pltpu.make_async_copy(src, dst, out_sem.at[i])
 
@@ -396,7 +410,8 @@
             pltpu.VMEM((2, own, 128), jnp.float32),
             pltpu.VMEM((2, 3, own, 128), jnp.float32),
             pltpu.VMEM((2, 3, own, 128), jnp.float32),
-            pltpu.VMEM((2, own, 128), jnp.bfloat16),
+            pltpu.VMEM((total_rows, 128), jnp.bfloat16),
+            pltpu.VMEM((own, 128), jnp.bfloat16),
             pltpu.VMEM((8, 8, 128), jnp.float32),
             pltpu.VMEM((2, feats, 128), jnp.float32),
             pltpu.VMEM((2, n_mp, feats, 128), jnp.float32),
@@ -473,44 +488,47 @@
     )(coefs, g, master, momenta, second, *earlier)
 
 
-def assemble_kernel(n_dp, own, full_ref, mine_ref, *rest):
-    count = 2 * (n_dp - 2)
+def assemble_kernel(n_dp, own, chunks, full_ref, mine_ref, *rest):
+    count = len(chunks)
     others = rest[:count]
     out_ref, fbuf, buf, load_sem, store_sem = rest[count:]
     z = lax.axis_index("dp")
     moves = [(full_ref, fbuf, out_ref.at[0, 0], None)]
     moves.append((mine_ref, buf.at[0], out_ref.at[0, 1, pl.ds(pl.multiple_of(z * own, STRIP), own)], None))
-    for i in range(count):
-        c = z - (i // 2 + 1) if i % 2 == 0 else z + (i // 2 + 1)
-        ok = (c >= 0) if i % 2 == 0 else (c < n_dp)
+    for i, chunk in enumerate(chunks):
+        c = chunk(z)
         at = pl.ds(pl.multiple_of(jnp.clip(c, 0, n_dp - 1) * own, STRIP), own)
-        moves.append((others[i], buf.at[1 + i], out_ref.at[0, 1, at], ok))
+        moves.append((others[i], buf.at[1 + i], out_ref.at[0, 1, at], (c >= 0) & (c < n_dp)))
 
     def each(act):
         for i, (src, mid, dst, ok) in enumerate(moves):
-            load = pltpu.make_async_copy(src, mid, load_sem.at[i])
-            store = pltpu.make_async_copy(mid, dst, store_sem.at[i])
+            def move(i=i, src=src, mid=mid, dst=dst):
+                act(
+                    functools.partial(pltpu.make_async_copy, src, mid, load_sem.at[i]),
+                    functools.partial(pltpu.make_async_copy, mid, dst, store_sem.at[i]),
+                )
+
             if ok is None:
-                act(load, store)
+                move()
             else:
-                pl.when(ok)(functools.partial(act, load, store))
-
-    each(lambda load, store: load.start())
+                pl.when(ok)(move)
+
+    each(lambda load, store: load().start())
 
     def forward(load, store):
-        load.wait()
-        store.start()
+        load().wait()
+        store().start()
 
     each(forward)
-    each(lambda load, store: store.wait())
-
-
-def assemble(n_dp, full, mine, others):
+    each(lambda load, store: store().wait())
+
+
+def assemble(n_dp, full, mine, others, chunks):
     own = mine.shape[0]
     anywhere = pl.BlockSpec(memory_space=pl.ANY)
     count = 2 + len(others)
     return pl.pallas_call(
-        functools.partial(assemble_kernel, n_dp, own),
+        functools.partial(assemble_kernel, n_dp, own, chunks),
         out_shape=jax.ShapeDtypeStruct((1, 2) + full.shape, full.dtype),
         in_specs=[anywhere] * count,
         out_specs=anywhere,
@@ -525,31 +543,31 @@
     )(full, mine, *others)
 
 
-def last_kernel(n_dp, own, right_ref, left_ref, _, out_ref, buf, sems):
+def last_kernel(n_dp, own, *rest):
+    out_ref, sem = rest[-2:]
     z = lax.axis_index("dp")
-    for d, (src, row) in enumerate(((right_ref, 0), (left_ref, (n_dp - 1) * own))):
-
-        @pl.when(z == (n_dp - 1 if d == 0 else 0))
-        def _():
-            load = pltpu.make_async_copy(src, buf, sems.at[0])
-            load.start()
-            load.wait()
-            store = pltpu.make_async_copy(buf, out_ref.at[0, 1, pl.ds(row, own)], sems.at[1])
+    for i, row in enumerate((0, (n_dp - 1) * own)):
+
+        @pl.when(z == (n_dp - 1 if i == 0 else 0))
+        def _():
+            src = rest[0] if i == 0 else rest[len(rest) - 4]
+            store = pltpu.make_async_copy(src, out_ref.at[0, 1, pl.ds(row, own)], sem)
             store.start()
             store.wait()
 
 
-def last(n_dp, right, left, out):
+def last(n_dp, arrived, out):
     anywhere = pl.BlockSpec(memory_space=pl.ANY)
     return pl.pallas_call(
-        functools.partial(last_kernel, n_dp, right.shape[0]),
+        functools.partial(last_kernel, n_dp, arrived[0].shape[0]),
         out_shape=jax.ShapeDtypeStruct(out.shape, out.dtype),
-        in_specs=[anywhere] * 3,
+        in_specs=[anywhere] * (len(arrived) + 1),
         out_specs=anywhere,
-        input_output_aliases={2: 0},
-        scratch_shapes=[pltpu.VMEM(right.shape, right.dtype), pltpu.SemaphoreType.DMA((2,))],
+        input_output_aliases={len(arrived): 0},
+        scratch_shapes=[pltpu.SemaphoreType.DMA],
+        compiler_params=pltpu.CompilerParams(vmem_limit_bytes=4 << 20),
         name="last",
-    )(right, left, out)
+    )(*arrived, out)
 
 
 def local(
@@ -560,17 +578,38 @@
         n_dp, n_mp, grad_parts, master, momenta, second, step_count, mlp_first, mlp_bias, mlp_second, tensor_weight
     )
     others = [right, left]
-    state = ()
-    for step in range(2, n_dp):
-        sent = (right, left)
-        right = lax.ppermute(sent[0], "dp", [(i, i + 1) for i in range(step - 1, n_dp - 1)])
-        left = lax.ppermute(sent[1], "dp", [(i, i - 1) for i in range(1, n_dp - step + 1)])
-        if step <= 3:
-            state = finish(step - 2, feats, hidden, coefs, g, master, momenta, second, state)
-        if step < n_dp - 1:
-            right, left, state = lax.optimization_barrier((right, left, state))
-            others += [right, left]
-    out = last(n_dp, right, left, assemble(n_dp, full0, p1, others))
+    net = (feats, hidden, coefs, g, master, momenta, second)
+    if n_dp == 4:
+        inner, outer = right, left
+        crossed = lax.ppermute(inner, "dp", [(1, 2), (2, 1)])
+        ended = lax.ppermute(outer, "dp", [(2, 3), (1, 0)])
+        state = finish(0, *net)
+        crossed, state = lax.optimization_barrier((crossed, state))
+        arrived = [lax.ppermute(crossed, "dp", [(2, 3), (1, 0)])]
+        state = finish(1, *net, state)
+        others += [crossed, ended]
+        none = -1
+        chunks = [
+            lambda z: jnp.where(z == 1, 0, jnp.where(z == 2, 3, none)),
+            lambda z: jnp.where(z < 2, z + 1, z - 1),
+            lambda z: jnp.where(z == 1, 3, jnp.where(z == 2, 0, none)),
+            lambda z: jnp.where(z == 0, 2, jnp.where(z == 3, 1, none)),
+        ]
+    else:
+        chunks = [lambda z: z - 1, lambda z: z + 1]
+        state = ()
+        for step in range(2, n_dp):
+            sent = (right, left)
+            right = lax.ppermute(sent[0], "dp", [(i, i + 1) for i in range(step - 1, n_dp - 1)])
+            left = lax.ppermute(sent[1], "dp", [(i, i - 1) for i in range(1, n_dp - step + 1)])
+            if step <= 3:
+                state = finish(step - 2, *net, state)
+            if step < n_dp - 1:
+                right, left, state = lax.optimization_barrier((right, left, state))
+                others += [right, left]
+                chunks += [lambda z, step=step: z - step, lambda z, step=step: z + step]
+        arrived = [right, left]
+    out = last(n_dp, arrived, assemble(n_dp, full0, p1, others, chunks))
     return (out, *state)
 
 

time: 288 us -> 283 us (0.983)
  waiting for transfers between devices: 12.6 us -> 8.88 us
    ppermute x4 -> x3, waiting for transfers between devices: 12.6 us -> 8.88 us  [the longest x1 8.88 us: local(): ended = lax.ppermute(outer, 'dp', [(2, 3), (1, 0)])]
  transfers between devices with their start and end apart: 4 -> 3, of which waited for: 2 -> 1; matrix products, arithmetic and copies ran while one was open for 0% -> 0% of each run, Pallas kernels for 15% -> 15%
where the time goes in v2:
time: 283 us
  Pallas kernels  268 us (95%)
  waiting for transfers between devices  8.88 us (3%)
  starting transfers between devices  3.32 us (1%)
    pallas_call x1, Pallas kernels, mega(): pl.pallas_call(functools.partial(mega_kernel, plan, feats, hidden), out_s...  224 us
    pallas_call x2, Pallas kernels, finish(): pl.pallas_call(functools.partial(finish_kernel, t, feats, hidden, coefs.s...  37 us
    ppermute x1, waiting for transfers between devices, local(): ended = lax.ppermute(outer, 'dp', [(2, 3), (1, 0)])  8.88 us
    pallas_call x1, Pallas kernels, assemble(): pl.pallas_call(functools.partial(assemble_kernel, n_dp, own, chunks), out...  5.71 us
  transfers between devices with their start and end apart: 3, of which 1 were waited for; matrix products, arithmetic and copies ran while one was open for 0% of the time, Pallas kernels for 15%

profile of v2, /device:TPU:0, one launch (start us, length us, event | category | flops | bytes accessed | tf_op | source)
XLA Modules:
  0.0 282.5 jit_solution(14187119922106661942)
XLA Ops:
  1.3 224.2 %exchange.1 = (bf16[18432,128]{1,0:T(8,128)(2,1)}, bf16[4608,128]{1,0:T(8,128)(2,1)}, bf16[4608,128]{1,0:T(8,128)(2,1)}, bf16[4608,128]{1,0:T(8,128)(2,1)}, bf16[2,4608,128]{2,1,0:T(8,128)(2,1)}, /*index=5*/f32[88]{0:T(128)}) custom-call(bf16[1,1,2,18432,128]{4,3,2,1,0:T(8,128)(2,1)} %grad_ref.1, f32[1,2,4608,128]{3,2,1,0:T(8,128)} %master_ref.5, ...), custom_call_target="tpu_custom_call" | custom-call | flops 1000000000 | bytes 100000000 | tf_op jit(solution)/shard_map/exchange/pallas_call | solution.py:395
  225.4 0.7 collective-permute-start
  226.2 1.3 collective-permute-start.2
  227.5 18.5 %finish0.1 = (f32[1,2,4608,128]{3,2,1,0:T(8,128)}, f32[3,1,2,4608,128]{4,3,2,1,0:T(8,128)}, f32[3,1,2,4608,128]{4,3,2,1,0:T(8,128)}, f32[1,2,4608,128]{3,2,1,0:T(8,128)}) custom-call(f32[88]{0:T(128)} %get-tuple-element.25.coef, bf16[2,4608,128]{2,1,0:T(8,128)(2,1)} %get-tuple-element.26.g_ref, f32[1,2,4608,128]{3,2,1,0:T(8,128)} %master_ref.5, ...), custom_call_target="tpu_custom_call" | custom-call | flops 76677120 | bytes 36569088 | tf_op jit(solution)/shard_map/finish0/pallas_call | solution.py:467
  246.0 0.0 collective-permute-done.rest_2_
  246.0 0.0 copy-start
  246.0 1.3 collective-permute-start.1
  247.3 8.9 %collective-permute-done.2.rest_3_ = bf16[4608,128]{1,0:T(8,128)(2,1)S(1)} collective-permute-done((bf16[4608,128]{1,0:T(8,128)(2,1)}, bf16[4608,128]{1,0:T(8,128)(2,1)S(1)}, u32[]{:S(2)}, u32[]{:S(2)}) %collective-permute-start.2) | collective-permute-done | bytes 1179680 | tf_op jit(solution)/shard_map/ppermute | solution.py:585
  256.2 0.0 copy-start.1
  256.2 0.0 copy-done
  256.2 1.0 copy-done.1
  257.2 5.7 %assemble.1.rest_1_ = bf16[1,2,18432,128]{3,2,1,0:T(8,128)(2,1)} custom-call(bf16[18432,128]{1,0:T(8,128)(2,1)} %get-tuple-element.32.full_ref, bf16[4608,128]{1,0:T(8,128)(2,1)} %get-tuple-element.33.mine_ref, bf16[4608,128]{1,0:T(8,128)(2,1)} %get-tuple-element.24.rest_0_, bf16[4608,128]{1,0:T(8,128)(2,1)} %get-tuple-element.34.rest_1_, ...), custom_call_target="tpu_custom_call" | custom-call | flops 10000000 | bytes 9437184 | tf_op jit(solution)/shard_map/assemble/pallas_call | solution.py:530
  263.0 18.5 %finish1.1 = (f32[1,2,4608,128]{3,2,1,0:T(8,128)}, f32[3,1,2,4608,128]{4,3,2,1,0:T(8,128)}, f32[3,1,2,4608,128]{4,3,2,1,0:T(8,128)}, f32[1,2,4608,128]{3,2,1,0:T(8,128)}) custom-call(f32[88]{0:T(128)} %get-tuple-element.25.coef, ...), custom_call_target="tpu_custom_call", output_to_operand_aliasing={{0}: (5, {}), {1}: (6, {}), {2}: (7, {}), {3}: (8, {})} | custom-call | flops 76677120 | bytes 36569088 | tf_op jit(solution)/shard_map/finish1/pallas_call | solution.py:467
  281.5 0.0 collective-permute-done.1.rest_0_
  281.5 1.0 last.1
Async XLA Ops:
  225.4 20.6 %collective-permute-start = (bf16[4608,128]{1,0:T(8,128)(2,1)}, bf16[4608,128]{1,0:T(8,128)(2,1)S(1)}, u32[]{:S(2)}, u32[]{:S(2)}) collective-permute-start(bf16[4608,128]{1,0:T(8,128)(2,1)} %get-tuple-element.24.rest_0_), channel_id=1, source_target_pairs={{8,16},{16,8},{9,17},{17,9},{10,18},{18,10},{11,19},{19,11},{12,20... | collective-permute-start | bytes 3538952 | tf_op jit(solution)/shard_map/ppermute | solution.py:584
  226.2 30.0 %collective-permute-start.2 = (bf16[4608,128]{1,0:T(8,128)(2,1)}, bf16[4608,128]{1,0:T(8,128)(2,1)S(1)}, u32[]{:S(2)}, u32[]{:S(2)}) collective-permute-start(bf16[4608,128]{1,0:T(8,128)(2,1)} %get-tuple-element.34.rest_1_), channel_id=1, source_target_pairs={{16,24},{8,0},{17,25},{9,1},{18,26},{10,2},{19,27},{11,3},{20,28},... | collective-permute-start | bytes 3538952 | tf_op jit(solution)/shard_map/ppermute | solution.py:585
  246.0 10.2 %copy-start = (bf16[4608,128]{1,0:T(8,128)(2,1)}, bf16[4608,128]{1,0:T(8,128)(2,1)S(1)}, u32[]{:S(2)}) copy-start(bf16[4608,128]{1,0:T(8,128)(2,1)S(1)} %collective-permute-done.rest_2_) | copy-start | bytes 3538948
  246.0 35.5 %collective-permute-start.1 = (bf16[4608,128]{1,0:T(8,128)(2,1)S(1)}, bf16[4608,128]{1,0:T(8,128)(2,1)S(1)}, u32[]{:S(2)}, u32[]{:S(2)}) collective-permute-start(bf16[4608,128]{1,0:T(8,128)(2,1)S(1)} %collective-permute-done.rest_2_), channel_id=1, source_target_pairs={{16,24},{8,0},{17,25},{9,1},{18,26},{10,2},{19,27},{11,3},{20,28},... | collective-permute-start | bytes 3538952 | tf_op jit(solution)/shard_map/ppermute | solution.py:588
  256.2 1.0 copy-start.1

commit v3 on v2

--- a/solution.py
+++ b/solution.py
@@ -13,6 +13,7 @@
 LAG = 3
 DEPTH = 4
 MOST = 16
+BLOCK = 1152
 
 
 def block_rows(rows, most=1152):
@@ -115,12 +116,8 @@
     order = []
     for i in range((n + 1) // 2):
         order += [n - 1 - i] + ([i] if i != n - 1 - i else [])
-    for t in range(2):
-        for c in order:
-            chunk_load(t, c).start()
-    for t in range(2):
-        for copy in state_loads(t):
-            copy.start()
+    for c in order[:2]:
+        chunk_load(0, c).start()
 
     barrier = pltpu.get_barrier_semaphore()
     for j in range(1, m_n):
@@ -212,6 +209,20 @@
                 @pl.when(active & late & (q < n - 1) & chosen)
                 def _():
                     remote(d, pbuf.at[piece(0, k)], sides[side].at[piece(0, k)], tau).start()
+
+        @pl.when(T == 0)
+        def _():
+            for c in order[2:]:
+                chunk_load(0, c).start()
+            for c in order:
+                chunk_load(1, c).start()
+
+        for t in range(2):
+
+            @pl.when(T == 2 + 2 * t)
+            def _():
+                for copy in state_loads(t):
+                    copy.start()
 
         for d in range(2):
             edge = 0 if d == 0 else n - 1
@@ -437,9 +448,10 @@
 
 def finish_kernel(t, feats, hidden, width, coef, g_ref, master_ref, mom_ref, sec_ref, *rest):
     nm_ref, nmom_ref, nsec_ref, up_ref = rest[-4:]
+    part = 64 if g_ref.shape[1] % 64 == 0 else STRIP
 
     def body(k, carry):
-        rows = pl.ds(pl.multiple_of(k * STRIP, STRIP), STRIP)
+        rows = pl.ds(pl.multiple_of(k * part, part), part)
         g = g_ref[0, rows, :].astype(jnp.float32)
         moments, squares = advanced(
             g, [mom_ref[c, 0, 0, rows, :] for c in range(3)], [sec_ref[c, 0, 0, rows, :] for c in range(3)]
@@ -453,12 +465,12 @@
         nm_ref[0, 0, rows, :] = master - 0.05 * update
         return carry
 
-    lax.fori_loop(0, g_ref.shape[1] // STRIP, body, 0)
+    lax.fori_loop(0, g_ref.shape[1] // part, body, 0)
 
 
 def finish(t, feats, hidden, coefs, g, master, momenta, second, earlier=()):
     own = g.shape[1]
-    rows = block_rows(own)
+    rows = block_rows(own, BLOCK)
     specs = [
         pl.BlockSpec((1, 1, rows, 128), lambda i: (0, t, i, 0)),
         pl.BlockSpec((3, 1, 1, rows, 128), lambda i: (0, 0, t, i, 0)),

time: 283 us -> 282 us (level)
  transfers between devices with their start and end apart: 3 -> 3, of which waited for: 1 -> 2; matrix products, arithmetic and copies ran while one was open for 0% -> 0% of each run, Pallas kernels for 15% -> 14%
where the time goes in v3:
time: 282 us
  Pallas kernels  266 us (94%)
  waiting for transfers between devices  10.7 us (4%)
  starting transfers between devices  3.32 us (1%)
    pallas_call x1, Pallas kernels, mega(): pl.pallas_call(functools.partial(mega_kernel, plan, feats, hidden), out_s...  224 us
    pallas_call x2, Pallas kernels, finish(): pl.pallas_call(functools.partial(finish_kernel, t, feats, hidden, coefs.s...  34.7 us
    ppermute x1, waiting for transfers between devices, local(): ended = lax.ppermute(outer, 'dp', [(2, 3), (1, 0)])  10 us
    pallas_call x1, Pallas kernels, assemble(): pl.pallas_call(functools.partial(assemble_kernel, n_dp, own, chunks), out...  5.71 us
  transfers between devices with their start and end apart: 3, of which 2 were waited for; matrix products, arithmetic and copies ran while one was open for 0% of the time, Pallas kernels for 14%

profile of v3, /device:TPU:0, one launch (start us, length us, event | category | flops | bytes accessed | tf_op | source)
XLA Modules:
  0.0 282.0 jit_solution(14011393607278764403)
XLA Ops:
  1.3 224.1 %exchange.1 = (bf16[18432,128]{1,0:T(8,128)(2,1)}, bf16[4608,128]{1,0:T(8,128)(2,1)}, bf16[4608,128]{1,0:T(8,128)(2,1)}, bf16[4608,128]{1,0:T(8,128)(2,1)}, bf16[2,4608,128]{2,1,0:T(8,128)(2,1)}, /*index=5*/f32[88]{0:T(128)}) custom-call(bf16[1,1,2,18432,128]{4,3,2,1,0:T(8,128)(2,1)} %grad_ref.1, f32[1,2,4608,128]{3,2,1,0:T(8,128)} %master_ref.5, ...), custom_call_target="tpu_custom_call" | custom-call | flops 1000000000 | bytes 100000000 | tf_op jit(solution)/shard_map/exchange/pallas_call | solution.py:406
  225.4 0.7 collective-permute-start
  226.2 1.3 collective-permute-start.2
  227.5 17.4 %finish0.1 = (f32[1,2,4608,128]{3,2,1,0:T(8,128)}, f32[3,1,2,4608,128]{4,3,2,1,0:T(8,128)}, f32[3,1,2,4608,128]{4,3,2,1,0:T(8,128)}, f32[1,2,4608,128]{3,2,1,0:T(8,128)}) custom-call(f32[88]{0:T(128)} %get-tuple-element.25.coef, bf16[2,4608,128]{2,1,0:T(8,128)(2,1)} %get-tuple-element.26.g_ref, f32[1,2,4608,128]{3,2,1,0:T(8,128)} %master_ref.5, ...), custom_call_target="tpu_custom_call" | custom-call | flops 76677120 | bytes 36569088 | tf_op jit(solution)/shard_map/finish0/pallas_call | solution.py:479
  244.8 0.0 collective-permute-done.rest_2_
  244.8 0.0 copy-start
  244.8 1.3 collective-permute-start.1
  246.1 10.0 %collective-permute-done.2.rest_3_ = bf16[4608,128]{1,0:T(8,128)(2,1)S(1)} collective-permute-done((bf16[4608,128]{1,0:T(8,128)(2,1)}, bf16[4608,128]{1,0:T(8,128)(2,1)S(1)}, u32[]{:S(2)}, u32[]{:S(2)}) %collective-permute-start.2) | collective-permute-done | bytes 1179680 | tf_op jit(solution)/shard_map/ppermute | solution.py:597
  256.2 0.0 copy-start.1
  256.2 0.0 copy-done
  256.2 1.0 copy-done.1
  257.2 5.7 %assemble.1.rest_1_ = bf16[1,2,18432,128]{3,2,1,0:T(8,128)(2,1)} custom-call(bf16[18432,128]{1,0:T(8,128)(2,1)} %get-tuple-element.32.full_ref, bf16[4608,128]{1,0:T(8,128)(2,1)} %get-tuple-element.33.mine_ref, bf16[4608,128]{1,0:T(8,128)(2,1)} %get-tuple-element.24.rest_0_, bf16[4608,128]{1,0:T(8,128)(2,1)} %get-tuple-element.34.rest_1_, ...), custom_call_target="tpu_custom_call" | custom-call | flops 10000000 | bytes 9437184 | tf_op jit(solution)/shard_map/assemble/pallas_call | solution.py:542
  263.0 17.3 %finish1.1 = (f32[1,2,4608,128]{3,2,1,0:T(8,128)}, f32[3,1,2,4608,128]{4,3,2,1,0:T(8,128)}, f32[3,1,2,4608,128]{4,3,2,1,0:T(8,128)}, f32[1,2,4608,128]{3,2,1,0:T(8,128)}) custom-call(f32[88]{0:T(128)} %get-tuple-element.25.coef, ...), custom_call_target="tpu_custom_call", output_to_operand_aliasing={{0}: (5, {}), {1}: (6, {}), {2}: (7, {}), {3}: (8, {})} | custom-call | flops 76677120 | bytes 36569088 | tf_op jit(solution)/shard_map/finish1/pallas_call | solution.py:479
  280.3 0.7 collective-permute-done.1.rest_0_
  281.0 1.0 last.1
Async XLA Ops:
  225.4 19.4 %collective-permute-start = (bf16[4608,128]{1,0:T(8,128)(2,1)}, bf16[4608,128]{1,0:T(8,128)(2,1)S(1)}, u32[]{:S(2)}, u32[]{:S(2)}) collective-permute-start(bf16[4608,128]{1,0:T(8,128)(2,1)} %get-tuple-element.24.rest_0_), channel_id=1, source_target_pairs={{8,16},{16,8},{9,17},{17,9},{10,18},{18,10},{11,19},{19,11},{12,20... | collective-permute-start | bytes 3538952 | tf_op jit(solution)/shard_map/ppermute | solution.py:596
  226.2 30.0 %collective-permute-start.2 = (bf16[4608,128]{1,0:T(8,128)(2,1)}, bf16[4608,128]{1,0:T(8,128)(2,1)S(1)}, u32[]{:S(2)}, u32[]{:S(2)}) collective-permute-start(bf16[4608,128]{1,0:T(8,128)(2,1)} %get-tuple-element.34.rest_1_), channel_id=1, source_target_pairs={{16,24},{8,0},{17,25},{9,1},{18,26},{10,2},{19,27},{11,3},{20,28},... | collective-permute-start | bytes 3538952 | tf_op jit(solution)/shard_map/ppermute | solution.py:597
  244.8 11.4 %copy-start = (bf16[4608,128]{1,0:T(8,128)(2,1)}, bf16[4608,128]{1,0:T(8,128)(2,1)S(1)}, u32[]{:S(2)}) copy-start(bf16[4608,128]{1,0:T(8,128)(2,1)S(1)} %collective-permute-done.rest_2_) | copy-start | bytes 3538948
  244.8 36.1 %collective-permute-start.1 = (bf16[4608,128]{1,0:T(8,128)(2,1)S(1)}, bf16[4608,128]{1,0:T(8,128)(2,1)S(1)}, u32[]{:S(2)}, u32[]{:S(2)}) collective-permute-start(bf16[4608,128]{1,0:T(8,128)(2,1)S(1)} %collective-permute-done.rest_2_), channel_id=1, source_target_pairs={{16,24},{8,0},{17,25},{9,1},{18,26},{10,2},{19,27},{11,3},{20,28},... | collective-permute-start | bytes 3538952 | tf_op jit(solution)/shard_map/ppermute | solution.py:600
  256.2 1.0 copy-start.1
